TPU v7x, 32 devices: a whole 2x2x4 slice. The times are simulated.
32 devices in a mesh: facet: 4 (over z), sub: 2 (over x), base: 4 (over y, core).
Axes of the slice: x: 2, y: 2, z: 4, core: 2. Of those that a mesh axis runs over, the one named last changes fastest.
Arguments:
- sky_image: bfloat16 [16384, 1024], P(('facet', 'base')), may hold values from -6 to 6
- facet_rows: int32 [4], replicated, may hold values from 0 to 126976
- column_offset: int32 [1], replicated, may hold values from 0 to 130816
- subgrid_offsets: int32 [2], replicated, may hold values from 0 to 130816
- vis_u: int32 [2, 32768], P('sub', ('facet', 'base')), may hold values from 0 to 1023
- vis_v: int32 [2, 32768], P('sub', ('facet', 'base')), may hold values from 0 to 1023
- observed: float32 [2, 2, 32768], P('sub', None, ('facet', 'base')), may hold values from -6 to 6
- weights: float32 [2, 32768], P('sub', ('facet', 'base')), may hold values from 0.3 to 3
- block_counts: int32 [2, 16], P('sub', ('facet', 'base')), may hold values from 1 to 16
Outputs:
- residual: float32 [2, 2, 32768], P('sub', None, ('facet', 'base'))
- facet_update: bfloat16 [16384, 1024], P(('facet', 'base'), 'sub')
Inputs may be any that keep to these rules, and one draw needn't show every extreme that they name: `block_counts`: the live blocks of a shard are its first ones.
All inputs are finite; a program needn't handle non-finite values.
Results may differ from a plain program's by a relative error of at most 0.008.
Values may be sent and summed in bfloat16 or wider, within the bound.
A program may use at most 64 MiB of HBM per device.

v0:
```python
import functools
import math

import jax
import jax.numpy as jnp
from jax import lax
from jax.experimental import pallas as pl
from jax.experimental.pallas import tpu as pltpu
from jax.sharding import PartitionSpec as P

NIMG = 131072
M = 256
SUBW = 1024
BLOCK = 128
MESH = pl.DeviceIdType.MESH
F32 = jnp.float32
BF16 = jnp.bfloat16


def unit(first, second, period):
    half = period // 2
    turn = ((first * second + half) & (period - 1)) - half
    y = turn.astype(F32) * (math.pi / period)
    q = y * y
    s = F32(-1.0 / 39916800.0)
    for k in (362880.0, -5040.0, 120.0, -6.0):
        s = s * q + F32(1.0 / k)
    s = (s * q + F32(1.0)) * y
    c = F32(1.0 / 479001600.0)
    for k in (-3628800.0, 40320.0, -720.0, 24.0, -2.0):
        c = c * q + F32(1.0 / k)
    c = c * q + F32(1.0)
    return F32(1.0) - F32(2.0) * s * s, F32(2.0) * s * c


def rows_iota(count, step=1):
    return lax.broadcasted_iota(jnp.int32, (count, 1), 0) * step


def lanes_iota(count):
    return lax.broadcasted_iota(jnp.int32, (1, count), 1)


def phase_product(coarse, fine, put):
    coarse_cos, coarse_sin = coarse
    fine_cos, fine_sin = fine
    for a in range(coarse_cos.shape[0]):
        ca, sa = coarse_cos[a : a + 1, :], coarse_sin[a : a + 1, :]
        put(a, ca * fine_cos - sa * fine_sin, sa * fine_cos + ca * fine_sin)


def pieces(groups, cols):
    row_blocks = min(groups, M // 16)
    col_blocks = groups // row_blocks
    height, width = M // row_blocks, cols // col_blocks
    return [
        (r * col_blocks + c, r * height, c * width, height, width)
        for r in range(row_blocks)
        for c in range(col_blocks)
    ]


def kernel(
    sizes,
    facet_rows,
    column_offset,
    subgrid_offsets,
    counts,
    sky_hbm,
    vis_u,
    vis_v,
    observed,
    weights,
    residual_out,
    update_out,
    sky,
    t1,
    spec,
    t2,
    du,
    dv,
    t5,
    t6,
    lhs,
    acc,
    zed,
    s_a,
    r_a,
    r_b,
    s_c,
    r_c,
    r_d,
    sky_sem,
    send_sem,
    recv_sem,
):
    n_facet, n_sub, n_base = sizes
    groups = n_facet * n_base
    total = groups * n_sub
    rows, columns = sky.shape
    vis = vis_u.shape[1]
    local_cols = update_out.shape[1]
    facet, sub, base = lax.axis_index("facet"), lax.axis_index("sub"), lax.axis_index("base")
    me = facet * n_base + base
    everyone = sub * groups + me

    def member(index):
        return {"facet": index // n_base, "sub": sub, "base": lax.rem(index, n_base)}

    def anyone(index):
        inside = lax.rem(index, groups)
        return {
            "facet": inside // n_base,
            "sub": index // groups,
            "base": lax.rem(inside, n_base),
        }

    fetch = pltpu.make_async_copy(sky_hbm, sky, sky_sem)
    fetch.start()
    barrier = pltpu.get_barrier_semaphore()

    @pl.loop(1, total)
    def _(j):
        pl.semaphore_signal(
            barrier,
            inc=1,
            device_id=anyone(lax.rem(everyone + j, total)),
            device_id_type=MESH,
        )

    def wait_all(phase, buffer, count):
        whole = buffer.at[pl.ds(0, count)]
        done = pltpu.make_async_remote_copy(
            whole, whole, send_sem.at[phase], recv_sem.at[phase], member(me), MESH
        )
        done.wait_recv()
        done.wait_send()

    def scatter(phase, source, landing):
        @pl.loop(1, groups)
        def _(j):
            other = lax.rem(me + j, groups)
            pltpu.make_async_remote_copy(
                source.at[other],
                landing.at[me],
                send_sem.at[phase],
                recv_sem.at[phase],
                member(other),
                MESH,
            ).start()

        landing[me] = source[me]

    def gather(phase, buffer, slot, own, count, where):
        @pl.loop(1, count)
        def _(j):
            pltpu.make_async_remote_copy(
                buffer.at[slot],
                buffer.at[slot],
                send_sem.at[phase],
                recv_sem.at[phase],
                where(lax.rem(own + j, count)),
                MESH,
            ).start()

    def summed(landing):
        result = landing[0].astype(F32)
        for g in range(1, groups):
            result = result + landing[g].astype(F32)
        return result

    freq = column_offset[0] + lanes_iota(M)
    high = 128
    coarse = unit(rows_iota(columns // high, high), freq, NIMG)
    fine = unit(rows_iota(high), freq, NIMG)
    norm = F32(columns ** (-0.5))

    def put_t1(a, c, s):
        t1[a * high : (a + 1) * high, :M] = (c * norm).astype(BF16)
        t1[a * high : (a + 1) * high, M:] = (s * -norm).astype(BF16)

    phase_product(coarse, fine, put_t1)

    row_start = facet_rows[facet] + base * rows
    positions = row_start + lanes_iota(rows)
    own_offset = subgrid_offsets[sub]
    step = 32
    coarse = unit(own_offset + rows_iota(M // step, step), positions, NIMG)
    fine = unit(rows_iota(step), positions, NIMG)

    def put_t2(a, c, s):
        t2[a * step : (a + 1) * step, :rows] = c.astype(BF16)
        t2[a * step : (a + 1) * step, rows:] = s.astype(BF16)

    phase_product(coarse, fine, put_t2)
    fetch.wait()

    tile = min(256, rows)

    @pl.loop(0, rows // tile)
    def _(i):
        here = pl.ds(pl.multiple_of(i * tile, tile), tile)
        there = pl.ds(pl.multiple_of(rows + i * tile, tile), tile)
        part = jnp.dot(sky[here, :], t1[...], preferred_element_type=F32)
        real, imag = part[:, :M].astype(BF16), part[:, M:].astype(BF16)
        spec[here, :M] = real
        spec[here, M:] = imag
        spec[there, :M] = imag
        spec[there, M:] = -real

    def split(source, target, scale):
        blocks = pieces(groups, 2 * M)
        for g, r, c, height, width in blocks:
            target[g] = (source[r : r + height, c : c + width] * scale).astype(BF16)

    acc[:M, :] = jnp.dot(t2[...], spec[...], preferred_element_type=F32)
    split(acc, s_a, F32((rows * groups) ** (-0.5)))

    pl.semaphore_wait(barrier, total - 1)
    scatter(0, s_a, r_a)

    fan = 16

    def grid_table(position, table):
        width = 512
        for at in range(0, vis, width):
            lanes = slice(at, at + width)
            place = position[0:1, lanes]
            coarse = unit(rows_iota(M // fan, fan), place, SUBW)
            fine = unit(rows_iota(fan), place, SUBW)

            def put(a, c, s):
                table[a * fan : (a + 1) * fan, lanes] = c.astype(BF16)
                table[M + a * fan : M + (a + 1) * fan, lanes] = s.astype(BF16)

            phase_product(coarse, fine, put)

    grid_table(vis_u, du)
    wait_all(0, r_a, groups - 1)
    r_b[me] = summed(r_a).astype(BF16)
    gather(1, r_b, me, me, groups, member)
    grid_table(vis_v, dv)
    wait_all(1, r_b, groups - 1)

    for g, r, c, height, width in pieces(groups, 2 * M):
        block = r_b[g]
        part = min(width, M)
        for inner in range(0, width, part):
            value = block[:, inner : inner + part]
            at = c + inner
            lhs[r : r + height, at : at + part] = value
            if at < M:
                lhs[M + r : M + r + height, M + at : M + at + part] = -value
            else:
                lhs[M + r : M + r + height, at - M : at - M + part] = value

    chunk = 512
    acc[...] = jnp.zeros_like(acc)
    live = counts[0, 0] * BLOCK

    @pl.loop(0, vis // chunk)
    def _(i):
        lanes = pl.ds(pl.multiple_of(i * chunk, chunk), chunk)
        half = jnp.dot(lhs[...], du[:, lanes], preferred_element_type=F32)
        half_re, half_im = half[:M], half[M:]
        cos_v, sin_v = dv[:M, lanes].astype(F32), dv[M:, lanes].astype(F32)
        model_re = jnp.sum(cos_v * half_re + sin_v * half_im, axis=0, keepdims=True)
        model_im = jnp.sum(cos_v * half_im - sin_v * half_re, axis=0, keepdims=True)
        alive = lanes_iota(chunk) + i * chunk < live
        weight = weights[0:1, lanes]
        inv = F32(1.0 / M)
        res_re = jnp.where(alive, weight * (observed[0, 0:1, lanes] - model_re * inv), F32(0.0))
        res_im = jnp.where(alive, weight * (observed[0, 1:2, lanes] - model_im * inv), F32(0.0))
        residual_out[0, 0:1, lanes] = res_re
        residual_out[0, 1:2, lanes] = res_im
        r0 = res_re.astype(BF16).astype(F32)
        r1 = res_im.astype(BF16).astype(F32)
        cos_u, sin_u = du[:M, lanes].astype(F32), du[M:, lanes].astype(F32)
        spread = jnp.concatenate(
            [(cos_u * r0 - sin_u * r1).astype(BF16), (sin_u * r0 + cos_u * r1).astype(BF16)],
            axis=0,
        )
        acc[...] += lax.dot_general(
            dv[:, lanes], spread, (((1,), (1,)), ((), ())), preferred_element_type=F32
        )

    acc[:M, :M] = acc[:M, :M] - acc[M:, M:]
    acc[:M, M:] = acc[:M, M:] + acc[M:, :M]
    split(acc, s_c, F32((vis * groups) ** (-0.5)))
    scatter(2, s_c, r_c)

    for s in range(n_sub):
        freqs = subgrid_offsets[s] + lanes_iota(M)
        coarse = unit(row_start + rows_iota(rows // high, high), freqs, NIMG)
        fine = unit(rows_iota(high), freqs, NIMG)

        def put_t5(a, c, sine, at=2 * M * s):
            t5[a * high : (a + 1) * high, at : at + M] = c.astype(BF16)
            t5[a * high : (a + 1) * high, at + M : at + 2 * M] = sine.astype(BF16)

        phase_product(coarse, fine, put_t5)

    wait_all(2, r_c, groups - 1)
    r_d[everyone] = summed(r_c).astype(BF16)
    gather(3, r_d, everyone, everyone, total, anyone)

    out_cols = sub * local_cols + lanes_iota(local_cols)
    coarse = unit(column_offset[0] + rows_iota(M // step, step), out_cols, NIMG)
    fine = unit(rows_iota(step), out_cols, NIMG)
    out_norm = F32(M ** (-0.5))

    def put_t6(a, c, s):
        t6[a * step : (a + 1) * step, :] = (c * out_norm).astype(BF16)
        t6[M + a * step : M + (a + 1) * step, :] = (s * -out_norm).astype(BF16)

    phase_product(coarse, fine, put_t6)
    wait_all(3, r_d, total - 1)

    for s in range(n_sub):
        top = 2 * M * s
        for g, r, c, height, width in pieces(groups, 2 * M):
            block = r_d[s * groups + g]
            part = min(width, M)
            for inner in range(0, width, part):
                value = block[:, inner : inner + part]
                at = c + inner
                zed[top + r : top + r + height, at : at + part] = value
                low = top + M + r
                if at < M:
                    zed[low : low + height, M + at : M + at + part] = value
                else:
                    zed[low : low + height, at - M : at - M + part] = -value

    scale = F32((n_sub * M) ** (-0.5))

    @pl.loop(0, rows // tile)
    def _(i):
        here = pl.ds(pl.multiple_of(i * tile, tile), tile)
        part = jnp.dot(t5[here, :], zed[...], preferred_element_type=F32)
        share = (part * scale).astype(BF16)
        update_out[here, :] = jnp.dot(share, t6[...], preferred_element_type=F32).astype(BF16)


def shards(
    sizes,
    sky_image,
    facet_rows,
    column_offset,
    subgrid_offsets,
    vis_u,
    vis_v,
    observed,
    weights,
    block_counts,
):
    n_facet, n_sub, n_base = sizes
    groups = n_facet * n_base
    rows, columns = sky_image.shape
    vis = vis_u.shape[1]
    local_cols = columns // n_sub
    _, _, _, height, width = pieces(groups, 2 * M)[0]
    smem = pl.BlockSpec(memory_space=pltpu.SMEM)
    vmem = pl.BlockSpec(memory_space=pltpu.VMEM)
    block = (groups, height, width)
    return pl.pallas_call(
        functools.partial(kernel, sizes),
        out_shape=(
            jax.ShapeDtypeStruct(observed.shape, F32),
            jax.ShapeDtypeStruct((rows, local_cols), BF16),
        ),
        in_specs=[smem] * 4 + [pl.BlockSpec(memory_space=pl.ANY)] + [vmem] * 4,
        out_specs=(vmem, vmem),
        scratch_shapes=[
            pltpu.VMEM((rows, columns), BF16),
            pltpu.VMEM((columns, 2 * M), BF16),
            pltpu.VMEM((2 * rows, 2 * M), BF16),
            pltpu.VMEM((M, 2 * rows), BF16),
            pltpu.VMEM((2 * M, vis), BF16),
            pltpu.VMEM((2 * M, vis), BF16),
            pltpu.VMEM((rows, 2 * M * n_sub), BF16),
            pltpu.VMEM((2 * M, local_cols), BF16),
            pltpu.VMEM((2 * M, 2 * M), BF16),
            pltpu.VMEM((2 * M, 2 * M), F32),
            pltpu.VMEM((2 * M * n_sub, 2 * M), BF16),
            pltpu.VMEM(block, BF16),
            pltpu.VMEM(block, BF16),
            pltpu.VMEM(block, BF16),
            pltpu.VMEM(block, BF16),
            pltpu.VMEM(block, BF16),
            pltpu.VMEM((n_sub * groups, height, width), BF16),
            pltpu.SemaphoreType.DMA,
            pltpu.SemaphoreType.DMA((4,)),
            pltpu.SemaphoreType.DMA((4,)),
        ],
        compiler_params=pltpu.CompilerParams(
            collective_id=0, has_side_effects=True, vmem_limit_bytes=56 * 1024 * 1024
        ),
        name="column",
    )(
        facet_rows,
        column_offset,
        subgrid_offsets,
        block_counts,
        sky_image,
        vis_u,
        vis_v,
        observed,
        weights,
    )


def solution(mesh):
    sizes = (mesh.shape["facet"], mesh.shape["sub"], mesh.shape["base"])
    return jax.shard_map(
        functools.partial(shards, sizes),
        mesh=mesh,
        in_specs=(
            P(("facet", "base"), None),
            P(),
            P(),
            P(),
            P("sub", ("facet", "base")),
            P("sub", ("facet", "base")),
            P("sub", None, ("facet", "base")),
            P("sub", ("facet", "base")),
            P("sub", ("facet", "base")),
        ),
        out_specs=(P("sub", None, ("facet", "base")), P(("facet", "base"), "sub")),
        check_vma=False,
    )
```

profile of v0, /device:TPU:0, one launch (start us, length us, event | category | flops | bytes accessed | tf_op | source)
XLA Modules:
  0.0 56.1 jit_solution(4380493233837418759)
XLA Ops:
  1.9 50.6 %column.1 = (f32[1,2,2048]{2,1,0:T(2,128)}, bf16[1024,512]{1,0:T(8,128)(2,1)}) custom-call(s32[4]{0:T(128)} %facet_rows.1, s32[1]{0:T(128)S(6)} %copy.13.column_offset, s32[2]{0:T(128)} %subgrid_offsets.1, s32[1,1]{1,0:T(1,128)S(6)} %copy.14.counts, bf16[1024,1024]{1,0:T(8,128)(2,1)} %sky_hbm.1, s32[1,2048]{1,0:T(1,128)} %vis_u.1, s32[1,2048]{1,0:T(1,128)} %vis_v.1, ...), custom_call_target="tpu_custom_call" | custom-call | tf_op jit(solution)/shard_map/column/pallas_call | solution.py:365
  52.5 1.3 %copy.15 = f32[1,2,2048]{2,1,0:T(2,128)} copy(f32[1,2,2048]{2,1,0:T(2,128)} %get-tuple-element.4) | data formatting | bytes 32768
  53.9 2.3 %copy.16 = bf16[1024,512]{1,0:T(8,128)(2,1)} copy(bf16[1024,512]{1,0:T(8,128)(2,1)} %get-tuple-element.5) | data formatting | bytes 2097152
where the time goes:
time: 56.4 us; the launch traced here: 56.1 us
  Pallas kernels  50.6 us (90%)
  local copies, waits for them, and re-layouts  3.59 us (6%)
  between operations  1.93 us (3%)
    pallas_call x1, Pallas kernels, shards(): pl.pallas_call(functools.partial(kernel, sizes), out_shape=(jax.ShapeDtyp...  50.6 us
    unnamed x2, local copies, waits for them, and re-layouts  3.59 us

commit v1 on v0

--- a/solution.py
+++ b/solution.py
@@ -72,7 +72,8 @@
     observed,
     weights,
     residual_out,
-    update_out,
+    share_out,
+    t6,
     sky,
     t1,
     spec,
@@ -80,14 +81,15 @@
     du,
     dv,
     t5,
-    t6,
     lhs,
     acc,
     zed,
     s_a,
+    x_a,
     r_a,
     r_b,
     s_c,
+    x_c,
     r_c,
     r_d,
     sky_sem,
@@ -99,10 +101,28 @@
     total = groups * n_sub
     rows, columns = sky.shape
     vis = vis_u.shape[1]
-    local_cols = update_out.shape[1]
+    local_cols = t6.shape[1]
     facet, sub, base = lax.axis_index("facet"), lax.axis_index("sub"), lax.axis_index("base")
     me = facet * n_base + base
     everyone = sub * groups + me
+    pairs = n_base // 2
+    half_group, half_total = groups // 2, total // 2
+    parity = lax.rem(base, 2)
+    pair = facet * pairs + base // 2
+    pair_all = sub * half_group + pair
+    sibling = {"facet": facet, "sub": sub, "base": base + 1 - 2 * parity}
+
+    def slot_of(g):
+        f, b = g // n_base, g % n_base
+        return (b % 2) * half_group + f * pairs + b // 2
+
+    def like(index):
+        inside = lax.rem(index, half_group)
+        return {
+            "facet": inside // pairs,
+            "sub": index // half_group,
+            "base": lax.rem(inside, pairs) * 2 + parity,
+        }
 
     def member(index):
         return {"facet": index // n_base, "sub": sub, "base": lax.rem(index, n_base)}
@@ -136,22 +156,33 @@
         done.wait_recv()
         done.wait_send()
 
-    def scatter(phase, source, landing):
-        @pl.loop(1, groups)
+    def scatter(phase, source, extra, landing):
+        theirs = source.at[pl.ds((1 - parity) * half_group, half_group)]
+        swap = pltpu.make_async_remote_copy(
+            theirs, extra, send_sem.at[phase + 4], recv_sem.at[phase + 4], sibling, MESH
+        )
+        swap.start()
+        swap.wait()
+        for i in range(half_group):
+            at = parity * half_group + i
+            joint = source[at].astype(F32) + extra[i].astype(F32)
+            source[at] = joint.astype(BF16)
+
+        @pl.loop(1, half_group)
         def _(j):
-            other = lax.rem(me + j, groups)
+            other = lax.rem(pair + j, half_group)
             pltpu.make_async_remote_copy(
-                source.at[other],
-                landing.at[me],
+                source.at[parity * half_group + other],
+                landing.at[pair],
                 send_sem.at[phase],
                 recv_sem.at[phase],
-                member(other),
+                like(sub * half_group + other),
                 MESH,
             ).start()
 
-        landing[me] = source[me]
-
-    def gather(phase, buffer, slot, own, count, where):
+        landing[pair] = source[parity * half_group + pair]
+
+    def gather(phase, buffer, slot, own, start, count):
         @pl.loop(1, count)
         def _(j):
             pltpu.make_async_remote_copy(
@@ -159,13 +190,22 @@
                 buffer.at[slot],
                 send_sem.at[phase],
                 recv_sem.at[phase],
-                where(lax.rem(own + j, count)),
+                like(start + lax.rem(own + j, count)),
                 MESH,
             ).start()
 
+    def hand_over(phase, buffer, count):
+        wait_all(phase, buffer, count - 1)
+        mine = buffer.at[pl.ds(parity * count, count)]
+        relay = pltpu.make_async_remote_copy(
+            mine, mine, send_sem.at[phase + 4], recv_sem.at[phase + 4], sibling, MESH
+        )
+        relay.start()
+        relay.wait()
+
     def summed(landing):
         result = landing[0].astype(F32)
-        for g in range(1, groups):
+        for g in range(1, half_group):
             result = result + landing[g].astype(F32)
         return result
 
@@ -211,13 +251,13 @@
     def split(source, target, scale):
         blocks = pieces(groups, 2 * M)
         for g, r, c, height, width in blocks:
-            target[g] = (source[r : r + height, c : c + width] * scale).astype(BF16)
+            target[slot_of(g)] = (source[r : r + height, c : c + width] * scale).astype(BF16)
 
     acc[:M, :] = jnp.dot(t2[...], spec[...], preferred_element_type=F32)
     split(acc, s_a, F32((rows * groups) ** (-0.5)))
 
     pl.semaphore_wait(barrier, total - 1)
-    scatter(0, s_a, r_a)
+    scatter(0, s_a, x_a, r_a)
 
     fan = 16
 
@@ -236,14 +276,15 @@
             phase_product(coarse, fine, put)
 
     grid_table(vis_u, du)
-    wait_all(0, r_a, groups - 1)
-    r_b[me] = summed(r_a).astype(BF16)
-    gather(1, r_b, me, me, groups, member)
+    wait_all(0, r_a, half_group - 1)
+    slot = parity * half_group + pair
+    r_b[slot] = summed(r_a).astype(BF16)
+    gather(1, r_b, slot, pair, sub * half_group, half_group)
     grid_table(vis_v, dv)
-    wait_all(1, r_b, groups - 1)
+    hand_over(1, r_b, half_group)
 
     for g, r, c, height, width in pieces(groups, 2 * M):
-        block = r_b[g]
+        block = r_b[slot_of(g)]
         part = min(width, M)
         for inner in range(0, width, part):
             value = block[:, inner : inner + part]
@@ -287,7 +328,7 @@
     acc[:M, :M] = acc[:M, :M] - acc[M:, M:]
     acc[:M, M:] = acc[:M, M:] + acc[M:, :M]
     split(acc, s_c, F32((vis * groups) ** (-0.5)))
-    scatter(2, s_c, r_c)
+    scatter(2, s_c, x_c, r_c)
 
     for s in range(n_sub):
         freqs = subgrid_offsets[s] + lanes_iota(M)
@@ -300,9 +341,10 @@
 
         phase_product(coarse, fine, put_t5)
 
-    wait_all(2, r_c, groups - 1)
-    r_d[everyone] = summed(r_c).astype(BF16)
-    gather(3, r_d, everyone, everyone, total, anyone)
+    wait_all(2, r_c, half_group - 1)
+    slot_all = parity * half_total + pair_all
+    r_d[slot_all] = summed(r_c).astype(BF16)
+    gather(3, r_d, slot_all, pair_all, 0, half_total)
 
     out_cols = sub * local_cols + lanes_iota(local_cols)
     coarse = unit(column_offset[0] + rows_iota(M // step, step), out_cols, NIMG)
@@ -314,12 +356,13 @@
         t6[M + a * step : M + (a + 1) * step, :] = (s * -out_norm).astype(BF16)
 
     phase_product(coarse, fine, put_t6)
-    wait_all(3, r_d, total - 1)
+    hand_over(3, r_d, half_total)
 
     for s in range(n_sub):
         top = 2 * M * s
         for g, r, c, height, width in pieces(groups, 2 * M):
-            block = r_d[s * groups + g]
+            place = slot_of(g)
+            block = r_d[(place // half_group) * half_total + s * half_group + place % half_group]
             part = min(width, M)
             for inner in range(0, width, part):
                 value = block[:, inner : inner + part]
@@ -338,7 +381,7 @@
         here = pl.ds(pl.multiple_of(i * tile, tile), tile)
         part = jnp.dot(t5[here, :], zed[...], preferred_element_type=F32)
         share = (part * scale).astype(BF16)
-        update_out[here, :] = jnp.dot(share, t6[...], preferred_element_type=F32).astype(BF16)
+        share_out[here, :] = share
 
 
 def shards(
@@ -362,14 +405,16 @@
     smem = pl.BlockSpec(memory_space=pltpu.SMEM)
     vmem = pl.BlockSpec(memory_space=pltpu.VMEM)
     block = (groups, height, width)
-    return pl.pallas_call(
+    half_block = (groups // 2, height, width)
+    residual, share, table = pl.pallas_call(
         functools.partial(kernel, sizes),
         out_shape=(
             jax.ShapeDtypeStruct(observed.shape, F32),
-            jax.ShapeDtypeStruct((rows, local_cols), BF16),
+            jax.ShapeDtypeStruct((rows, 2 * M), BF16),
+            jax.ShapeDtypeStruct((2 * M, local_cols), BF16),
         ),
         in_specs=[smem] * 4 + [pl.BlockSpec(memory_space=pl.ANY)] + [vmem] * 4,
-        out_specs=(vmem, vmem),
+        out_specs=(vmem, vmem, vmem),
         scratch_shapes=[
             pltpu.VMEM((rows, columns), BF16),
             pltpu.VMEM((columns, 2 * M), BF16),
@@ -378,19 +423,20 @@
             pltpu.VMEM((2 * M, vis), BF16),
             pltpu.VMEM((2 * M, vis), BF16),
             pltpu.VMEM((rows, 2 * M * n_sub), BF16),
-            pltpu.VMEM((2 * M, local_cols), BF16),
             pltpu.VMEM((2 * M, 2 * M), BF16),
             pltpu.VMEM((2 * M, 2 * M), F32),
             pltpu.VMEM((2 * M * n_sub, 2 * M), BF16),
             pltpu.VMEM(block, BF16),
+            pltpu.VMEM(half_block, BF16),
+            pltpu.VMEM(half_block, BF16),
             pltpu.VMEM(block, BF16),
             pltpu.VMEM(block, BF16),
-            pltpu.VMEM(block, BF16),
-            pltpu.VMEM(block, BF16),
+            pltpu.VMEM(half_block, BF16),
+            pltpu.VMEM(half_block, BF16),
             pltpu.VMEM((n_sub * groups, height, width), BF16),
             pltpu.SemaphoreType.DMA,
-            pltpu.SemaphoreType.DMA((4,)),
-            pltpu.SemaphoreType.DMA((4,)),
+            pltpu.SemaphoreType.DMA((8,)),
+            pltpu.SemaphoreType.DMA((8,)),
         ],
         compiler_params=pltpu.CompilerParams(
             collective_id=0, has_side_effects=True, vmem_limit_bytes=56 * 1024 * 1024
@@ -407,6 +453,7 @@
         observed,
         weights,
     )
+    return residual, jnp.dot(share, table, preferred_element_type=F32).astype(BF16)
 
 
 def solution(mesh):

time: 56.4 us -> 47.8 us (0.85)
  Pallas kernels: 50.6 us -> 42 us
  matrix products: 0 us -> 3.04 us
  local copies, waits for them, and re-layouts: 3.59 us -> 0.61 us
    pallas_call x1, Pallas kernels: 50.6 us -> 42 us  [shards(): pl.pallas_call(functools.partial(kernel, sizes), out_shape=(jax.ShapeDtyp...]
    dot_general x0 -> x1, matrix products: none -> 3.04 us  [shards(): jnp.dot(share, table, preferred_element_type=F32).astype(BF16)]
    unnamed x2 -> x3, local copies, waits for them, and re-layouts: 3.59 us -> 0.61 us
where the time goes in v1:
time: 47.8 us; the launch traced here: 47.6 us
  Pallas kernels  42 us (88%)
  matrix products  3.04 us (6%)
  between operations  1.94 us (4%)
  local copies, waits for them, and re-layouts  0.61 us (1%)
    pallas_call x1, Pallas kernels, shards(): pl.pallas_call(functools.partial(kernel, sizes), out_shape=(jax.ShapeDtyp...  42 us
    dot_general x1, matrix products, shards(): jnp.dot(share, table, preferred_element_type=F32).astype(BF16)  3.04 us

profile of v1, /device:TPU:0, one launch (start us, length us, event | category | flops | bytes accessed | tf_op | source)
XLA Modules:
  0.0 47.6 jit_solution(2159987750262701178)
XLA Ops:
  1.9 42.0 %column.1 = (f32[1,2,2048]{2,1,0:T(2,128)}, bf16[1024,512]{1,0:T(8,128)(2,1)}, bf16[512,512]{1,0:T(8,128)(2,1)}) custom-call(s32[4]{0:T(128)} %facet_rows.1, s32[1]{0:T(128)S(6)} %copy.12.column_offset, s32[2]{0:T(128)} %subgrid_offsets.1, s32[1,1]{1,0:T(1,128)S(6)} %copy.13.counts, bf16[1024,1024]{1,0:T(8,128)(2,1)} %sky_hbm.1, s32[1,2048]{1,0:T(1,128)} %vis_u.1, ...), custom_call_target="tpu_custom_call" | custom-call | tf_op jit(solution)/shard_map/column/pallas_call | solution.py:409
  43.9 0.0 copy-start
  43.9 3.0 %convolution_convert_fusion = bf16[1024,512]{1,0:T(8,128)(2,1)} fusion(bf16[1024,512]{1,0:T(8,128)(2,1)} %get-tuple-element.6, bf16[512,512]{1,0:T(8,128)(2,1)} %get-tuple-element.7), kind=kOutput, calls=%fused_computation | convolution fusion | flops 537395200 | bytes 2621440 | tf_op jit(solution)/shard_map/dot_general | solution.py:456
  46.9 0.0 copy-done
  46.9 0.6 %copy.14 = f32[1,2,2048]{2,1,0:T(2,128)} copy(f32[1,2,2048]{2,1,0:T(2,128)S(1)} %copy-done) | data formatting | bytes 32768
Async XLA Ops:
  43.9 3.0 %copy-start = (f32[1,2,2048]{2,1,0:T(2,128)S(1)}, f32[1,2,2048]{2,1,0:T(2,128)}, u32[]{:S(2)}) copy-start(f32[1,2,2048]{2,1,0:T(2,128)} %get-tuple-element.10) | copy-start | bytes 49156
